TPU v7x, 32 devices: a whole 2x2x4 slice. The times are simulated.
32 devices in a mesh: ctx: 8 (over z, y), tp: 4 (over x, core).
Axes of the slice: x: 2, y: 2, z: 4, core: 2. Of those that a mesh axis runs over, the one named last changes fastest.
Arguments:
- queries: bfloat16 [4096, 4096], P('ctx', 'tp'), may hold values from -22 to 22
- keys: bfloat16 [4096, 512], P('ctx', 'tp'), may hold values from -22 to 22
- values: bfloat16 [4096, 512], P('ctx', 'tp'), may hold values from -36 to 36
- positions: int32 [3, 4096], P(None, 'ctx'), may hold values from 0 to 4095
- segment_ids: int32 [4096], replicated, may hold values from 0 to 3, never falling along the last dimension, each value on 1 to 2048 neighbouring positions
- out_weight: bfloat16 [4096, 8192], P('tp', 'ctx'), may hold values from -0.09375 to 0.09375
- residual: bfloat16 [4096, 8192], P(('ctx', 'tp')), may hold values from -3 to 3
Outputs:
- layer_out: bfloat16 [4096, 8192], P(('ctx', 'tp'))
Inputs may be any that keep to these rules, and one draw needn't show every extreme that they name: `segment_ids`: ids never fall along the sequence; each document has 1 to 2048 tokens, and one has exactly 2048.
All inputs are finite; a program needn't handle non-finite values.
Results may differ from a plain program's by a relative error of at most 0.013.
Values may be sent and summed in bfloat16 or wider, within the bound.
A program may use at most 128 MiB of HBM per device.

v0:
```python
import math

import jax
import jax.numpy as jnp
from jax import lax
from jax.sharding import PartitionSpec as P

HD = 128
DOC = 2048


theta_base = 1000000.0


def from_behind(block, axis, distance):
    devices = range(lax.axis_size(axis))
    route = [(i - distance, i) for i in devices if i - distance in devices]
    return lax.ppermute(block, axis, route)


def rotary_tables(positions):
    half_dim = HD // 2
    freq_index = jnp.arange(half_dim)
    inv_freq = theta_base ** (-2.0 * freq_index.astype(jnp.float32) / HD)
    first_end = HD // 8
    second_end = first_end + 3 * HD // 16
    place = positions.astype(jnp.float32)
    chosen = jnp.where(
        freq_index[None, :] < first_end,
        place[0][:, None],
        jnp.where(freq_index[None, :] < second_end, place[1][:, None], place[2][:, None]),
    )
    angle = chosen * inv_freq[None, :]
    return (jnp.cos(angle), jnp.sin(angle))


def rotate(vectors, cosine_table, sine_table):
    half_dim = HD // 2
    lower_half = vectors[..., :half_dim]
    upper_half = vectors[..., half_dim:]
    cos_b = cosine_table[:, None, :]
    sin_b = sine_table[:, None, :]
    return jnp.concatenate(
        [lower_half * cos_b - upper_half * sin_b, upper_half * cos_b + lower_half * sin_b], axis=-1
    )


def on_device(queries, keys, values, positions, segment_ids, out_weight, residual):
    tok_rows = queries.shape[0]
    local_heads = queries.shape[1] // HD
    local_kv = keys.shape[1] // HD
    group_size = local_heads // local_kv
    reach_blocks = (DOC + tok_rows - 2) // tok_rows
    my_start = lax.axis_index("ctx") * tok_rows
    cosine_table, sine_table = rotary_tables(positions)
    rot_q = rotate(
        queries.reshape(tok_rows, local_heads, HD).astype(jnp.float32), cosine_table, sine_table
    ).astype(jnp.bfloat16)
    grouped = rot_q.reshape(tok_rows, local_kv, group_size, HD).transpose(1, 2, 0, 3)
    rot_k = rotate(
        keys.reshape(tok_rows, local_kv, HD).astype(jnp.float32), cosine_table, sine_table
    ).astype(jnp.bfloat16)
    key_flat = rot_k.reshape(tok_rows, local_kv * HD)
    query_index = my_start + jnp.arange(tok_rows, dtype=jnp.int32)
    query_seg = lax.dynamic_slice_in_dim(segment_ids, my_start, tok_rows, 0)
    score_scale = 1.0 / math.sqrt(HD)
    block_rows = math.gcd(tok_rows, 512)
    block_count = tok_rows // block_rows

    def absorb(running, stacked, offset):
        key_blocks = stacked[0].reshape(block_count, block_rows, local_kv, HD)
        value_blocks = stacked[1].reshape(block_count, block_rows, local_kv, HD)

        def advance(block_index, carried):
            key_block = lax.dynamic_index_in_dim(key_blocks, block_index, 0, keepdims=False)
            value_block = lax.dynamic_index_in_dim(value_blocks, block_index, 0, keepdims=False)
            key_first = offset + block_index * block_rows
            key_index = key_first + jnp.arange(block_rows, dtype=jnp.int32)
            key_seg = lax.dynamic_slice_in_dim(
                segment_ids, jnp.maximum(key_first, 0), block_rows, 0
            )
            allowed = (
                (key_index[None, :] <= query_index[:, None])
                & (key_index[None, :] >= 0)
                & (key_seg[None, :] == query_seg[:, None])
            )
            row_peak, row_sum, weighted = carried
            score = (
                jnp.einsum("kgtd,nkd->kgtn", grouped, key_block, preferred_element_type=jnp.float32)
                * score_scale
            )
            score = jnp.where(allowed, score, -1e30)
            new_peak = jnp.maximum(row_peak, jnp.max(score, axis=-1))
            prob = jnp.where(allowed, jnp.exp(score - new_peak[..., None]), 0.0)
            rescale = jnp.exp(row_peak - new_peak)
            row_sum = row_sum * rescale + jnp.sum(prob, axis=-1)
            weighted = weighted * rescale[..., None] + jnp.einsum(
                "kgtn,nkd->kgtd",
                prob.astype(jnp.bfloat16),
                value_block,
                preferred_element_type=jnp.float32,
            )
            return (new_peak, row_sum, weighted)

        return lax.fori_loop(0, block_count, advance, running)

    initial = (
        jnp.full((local_kv, group_size, tok_rows), -1e30, jnp.float32),
        jnp.zeros((local_kv, group_size, tok_rows), jnp.float32),
        jnp.zeros((local_kv, group_size, tok_rows, HD), jnp.float32),
    )
    own_pair = jnp.stack([key_flat, values], axis=0)
    state = absorb(initial, own_pair, my_start)

    def next_block(step_index, carried):
        moving, running = carried
        moving = from_behind(moving, "ctx", 1)
        running = absorb(running, moving, my_start - step_index * tok_rows)
        return (moving, running)

    moving, state = lax.fori_loop(1, reach_blocks + 1, next_block, (own_pair, state))
    row_peak, row_sum, weighted = state
    attended = (
        (weighted / row_sum[..., None])
        .transpose(2, 0, 1, 3)
        .reshape(tok_rows, local_heads * HD)
        .astype(jnp.bfloat16)
    )
    partial_sum = jnp.dot(
        attended,
        lax.all_gather(out_weight, "ctx", axis=1, tiled=True),
        preferred_element_type=jnp.float32,
    )
    partial_sum = partial_sum.astype(jnp.bfloat16).astype(jnp.float32)
    shared = lax.psum_scatter(
        partial_sum.astype(jnp.bfloat16), "tp", scatter_dimension=0, tiled=True
    ).astype(jnp.float32)
    return (shared + residual.astype(jnp.float32)).astype(jnp.bfloat16)


def solution(mesh):
    return jax.shard_map(
        on_device,
        mesh=mesh,
        in_specs=(
            P("ctx", "tp"),
            P("ctx", "tp"),
            P("ctx", "tp"),
            P(None, "ctx"),
            P(),
            P("tp", "ctx"),
            P(("ctx", "tp"), None),
        ),
        out_specs=P(("ctx", "tp"), None),
        check_vma=False,
    )
```

profile of v0, /device:TPU:5, one launch (start us, length us, event | category | flops | bytes accessed | tf_op | source)
XLA Modules:
  0.0 358.9 jit_solution(15099794177529089689)
XLA Ops:
  6.5 0.7 all-gather.2.cloned.1.call-update
  8.0 1.5 copy.11
  9.5 1.3 fusion.41
  10.8 1.8 copy.18
  12.6 1.9 copy.19
  14.6 0.8 fusion.42
  15.5 1.4 subtract_convert_fusion.1
  16.9 0.8 pad_maximum_fusion.1
  17.7 1.7 fusion.29
  19.4 2.5 fusion.24
  22.9 2.2 fusion.16
  25.1 2.0 fusion.18
  27.2 3.1 add_bitcast_fusion
  30.3 92.9 %while.28 = (s32[]{:T(128)}, bf16[2,512,128]{2,1,0:T(8,128)(2,1)}, f32[1,8,512]{2,1,0:T(8,128)S(1)}, f32[1,8,512]{2,1,0:T(8,128)S(1)}, f32[1,8,512,128]{3,2,1,0:...) while((s32[]{:T(128)}, bf16[2,512,128]{2,1,0:T(8,128)(2,1)}, ...), condition=%wide.region_5.6_spmd.clone.clone, body=%wide.region_2.5_spmd.clone.clone.sunk | while | flops 1103116288 | bytes 33572048 | solution.py:121
  30.5 3.1 collective-permute-start
  33.7 0.8 dynamic_slice.35
  34.8 11.6 %collective-permute-done = bf16[2,512,128]{2,1,0:T(8,128)(2,1)S(1)} collective-permute-done((bf16[2,512,128]{2,1,0:T(8,128)(2,1)}, bf16[2,512,128]{2,1,0:T(8,128)(2,1)S(1)}, u32[]{:S(2)}, u32[]{:S(2)}) %collective-permute-start) | collective-permute-done | bytes 262176 | tf_op jit(solution)/shard_map/while/body/eval_jaxpr/ppermute | solution.py:18
  46.5 1.5 fusion.51
  48.0 2.0 fusion.53
  50.1 0.7 copy.31
  50.8 3.1 bitcast_add_fusion.6
  53.9 4.0 %collective-permute-start = (bf16[2,512,128]{2,1,0:T(8,128)(2,1)}, bf16[2,512,128]{2,1,0:T(8,128)(2,1)S(1)}, u32[]{:S(2)}, u32[]{:S(2)}) collective-permute-start(bf16[2,512,128]{2,1,0:T(8,128)(2,1)} %get-tuple-element.443), channel_id=1, source_target_pairs={{0,4},{4,8},{8,12},{12,16},{16,20},{20,24},{24,28},{1,5},{5,9},{9,... | collective-permute-start | bytes 786440 | tf_op jit(solution)/shard_map/while/body/eval_jaxpr/ppermute | solution.py:18
  58.0 0.8 dynamic_slice.35
  59.1 10.4 %collective-permute-done = bf16[2,512,128]{2,1,0:T(8,128)(2,1)S(1)} collective-permute-done((bf16[2,512,128]{2,1,0:T(8,128)(2,1)}, bf16[2,512,128]{2,1,0:T(8,128)(2,1)S(1)}, u32[]{:S(2)}, u32[]{:S(2)}) %collective-permute-start) | collective-permute-done | bytes 262176 | tf_op jit(solution)/shard_map/while/body/eval_jaxpr/ppermute | solution.py:18
  69.5 1.5 fusion.51
  71.1 2.0 fusion.53
  73.1 0.7 copy.31
  73.9 3.1 bitcast_add_fusion.6
  77.0 5.0 %collective-permute-start = (bf16[2,512,128]{2,1,0:T(8,128)(2,1)}, bf16[2,512,128]{2,1,0:T(8,128)(2,1)S(1)}, u32[]{:S(2)}, u32[]{:S(2)}) collective-permute-start(bf16[2,512,128]{2,1,0:T(8,128)(2,1)} %get-tuple-element.443), channel_id=1, source_target_pairs={{0,4},{4,8},{8,12},{12,16},{16,20},{20,24},{24,28},{1,5},{5,9},{9,... | collective-permute-start | bytes 786440 | tf_op jit(solution)/shard_map/while/body/eval_jaxpr/ppermute | solution.py:18
  82.0 0.8 dynamic_slice.35
  83.2 10.2 %collective-permute-done = bf16[2,512,128]{2,1,0:T(8,128)(2,1)S(1)} collective-permute-done((bf16[2,512,128]{2,1,0:T(8,128)(2,1)}, bf16[2,512,128]{2,1,0:T(8,128)(2,1)S(1)}, u32[]{:S(2)}, u32[]{:S(2)}) %collective-permute-start) | collective-permute-done | bytes 262176 | tf_op jit(solution)/shard_map/while/body/eval_jaxpr/ppermute | solution.py:18
  93.4 1.5 fusion.51
  94.9 2.0 fusion.53
  97.0 0.7 copy.31
  97.7 3.1 bitcast_add_fusion.6
  100.9 9.8 %collective-permute-start = (bf16[2,512,128]{2,1,0:T(8,128)(2,1)}, bf16[2,512,128]{2,1,0:T(8,128)(2,1)S(1)}, u32[]{:S(2)}, u32[]{:S(2)}) collective-permute-start(bf16[2,512,128]{2,1,0:T(8,128)(2,1)} %get-tuple-element.443), channel_id=1, source_target_pairs={{0,4},{4,8},{8,12},{12,16},{16,20},{20,24},{24,28},{1,5},{5,9},{9,... | collective-permute-start | bytes 786440 | tf_op jit(solution)/shard_map/while/body/eval_jaxpr/ppermute | solution.py:18
  110.7 0.8 dynamic_slice.35
  111.8 4.0 %collective-permute-done = bf16[2,512,128]{2,1,0:T(8,128)(2,1)S(1)} collective-permute-done((bf16[2,512,128]{2,1,0:T(8,128)(2,1)}, bf16[2,512,128]{2,1,0:T(8,128)(2,1)S(1)}, u32[]{:S(2)}, u32[]{:S(2)}) %collective-permute-start) | collective-permute-done | bytes 262176 | tf_op jit(solution)/shard_map/while/body/eval_jaxpr/ppermute | solution.py:18
  115.8 1.5 fusion.51
  117.3 2.0 fusion.53
  119.4 0.7 copy.31
  120.1 3.1 bitcast_add_fusion.6
  123.3 1.3 copy-done.1
  124.6 1.9 copy.15
  126.8 131.5 %all-gather.2.cloned.1.call-done = bf16[1024,8192]{1,0:T(8,128)(2,1)} async-done(((bf16[1024,1024]{1,0:T(8,128)(2,1)}), bf16[1024,8192]{1,0:T(8,128)(2,1)}) %all-gather.2.cloned.1.call-update) | async-done | bytes 16777232 | tf_op jit(solution)/shard_map/all_gather | solution.py:131
  258.3 16.9 %convolution_convert_fusion = bf16[512,8192]{1,0:T(8,128)(2,1)} fusion(bf16[512,1024]{0,1:T(8,128)(2,1)S(1)} %bitcast.92, bf16[1024,8192]{1,0:T(8,128)(2,1)} %all-gather.2.cloned.1.call-done), kind=kOutput, calls=%fused_computation.24 | convolution fusion | flops 8594128896 | bytes 26214400 | tf_op jit(solution)/shard_map/dot_general | solution.py:129
  275.3 73.4 %reduce-scatter.2.cloned.1.call-done = bf16[128,8192]{1,0:T(8,128)(2,1)} async-done(((bf16[512,8192]{1,0:T(8,128)(2,1)}), bf16[128,8192]{1,0:T(8,128)(2,1)}) %reduce-scatter.2.cloned.1.call-update) | async-done | bytes 2097168 | tf_op jit(solution)/shard_map/reduce_scatter | solution.py:135
  348.7 3.4 add_convert_fusion
  (47 shorter events, 3.6 us)
Async XLA Ops:
  6.5 8.9 %copy-start.2 = (bf16[512,128]{1,0:T(8,128)(2,1)S(1)}, bf16[512,128]{1,0:T(8,128)(2,1)}, u32[]{:S(2)}) copy-start(bf16[512,128]{1,0:T(8,128)(2,1)} %param.10) | copy-start | bytes 393220
  6.5 10.3 %copy-start.3 = (bf16[512,128]{1,0:T(8,128)(2,1)S(1)}, bf16[512,128]{1,0:T(8,128)(2,1)}, u32[]{:S(2)}) copy-start(bf16[512,128]{1,0:T(8,128)(2,1)} %param.11) | copy-start | bytes 393220
  6.5 251.8 %all-gather.2.cloned.1.call-start = ((), (), s32[]{:S(2)}) async-start(), calls=%async_computation.1 | async-start | bytes 18874368 | tf_op jit(solution)/shard_map/all_gather | solution.py:131
  7.3 341.4 %reduce-scatter.2.cloned.1.call-start = ((), (), s32[]{:S(2)}) async-start(), calls=%async_computation.2 | async-start | bytes 10485760 | tf_op jit(solution)/shard_map/reduce_scatter | solution.py:135
  22.9 4.3 %copy-start.4 = (bf16[512,128]{1,0:T(8,128)(2,1)S(1)}, bf16[512,128]{1,0:T(8,128)(2,1)}, u32[]{:S(2)}) copy-start(bf16[512,128]{1,0:T(8,128)(2,1)} %param.11) | copy-start | bytes 393220
  30.5 16.0 %collective-permute-start = (bf16[2,512,128]{2,1,0:T(8,128)(2,1)}, bf16[2,512,128]{2,1,0:T(8,128)(2,1)S(1)}, u32[]{:S(2)}, u32[]{:S(2)}) collective-permute-start(bf16[2,512,128]{2,1,0:T(8,128)(2,1)} %get-tuple-element.443), channel_id=1, source_target_pairs={{0,4},{4,8},{8,12},{12,16},{16,20},{20,24},{24,28},{1,5},{5,9},{9,... | collective-permute-start | bytes 786440 | tf_op jit(solution)/shard_map/while/body/eval_jaxpr/ppermute | solution.py:18
  53.9 15.6 %collective-permute-start = (bf16[2,512,128]{2,1,0:T(8,128)(2,1)}, bf16[2,512,128]{2,1,0:T(8,128)(2,1)S(1)}, u32[]{:S(2)}, u32[]{:S(2)}) collective-permute-start(bf16[2,512,128]{2,1,0:T(8,128)(2,1)} %get-tuple-element.443), channel_id=1, source_target_pairs={{0,4},{4,8},{8,12},{12,16},{16,20},{20,24},{24,28},{1,5},{5,9},{9,... | collective-permute-start | bytes 786440 | tf_op jit(solution)/shard_map/while/body/eval_jaxpr/ppermute | solution.py:18
  77.0 16.4 %collective-permute-start = (bf16[2,512,128]{2,1,0:T(8,128)(2,1)}, bf16[2,512,128]{2,1,0:T(8,128)(2,1)S(1)}, u32[]{:S(2)}, u32[]{:S(2)}) collective-permute-start(bf16[2,512,128]{2,1,0:T(8,128)(2,1)} %get-tuple-element.443), channel_id=1, source_target_pairs={{0,4},{4,8},{8,12},{12,16},{16,20},{20,24},{24,28},{1,5},{5,9},{9,... | collective-permute-start | bytes 786440 | tf_op jit(solution)/shard_map/while/body/eval_jaxpr/ppermute | solution.py:18
  100.9 14.9 %collective-permute-start = (bf16[2,512,128]{2,1,0:T(8,128)(2,1)}, bf16[2,512,128]{2,1,0:T(8,128)(2,1)S(1)}, u32[]{:S(2)}, u32[]{:S(2)}) collective-permute-start(bf16[2,512,128]{2,1,0:T(8,128)(2,1)} %get-tuple-element.443), channel_id=1, source_target_pairs={{0,4},{4,8},{8,12},{12,16},{16,20},{20,24},{24,28},{1,5},{5,9},{9,... | collective-permute-start | bytes 786440 | tf_op jit(solution)/shard_map/while/body/eval_jaxpr/ppermute | solution.py:18
  123.3 1.3 copy-start.1
  275.3 73.4 %copy-start = (bf16[128,8192]{1,0:T(8,128)(2,1)S(1)}, bf16[128,8192]{1,0:T(8,128)(2,1)}, u32[]{:S(2)}) copy-start(bf16[128,8192]{1,0:T(8,128)(2,1)} %param.15) | copy-start | bytes 6291460
Sparse Core Ops, SparseCore 0:
  9.5 248.7 all-gather.1
  275.4 73.2 reduce-scatter.1
where the time goes:
time: 361 us; the launch traced here: 359 us
  waiting for transfers between devices  242 us (67%)
  matrix products  40.7 us (11%)
  other arithmetic  24.4 us (7%)
  starting transfers between devices  21.9 us (6%)
  local copies, waits for them, and re-layouts  15.7 us (4%)
  between operations  13.6 us (4%)
    all_gather x1, waiting for transfers between devices, on_device(): lax.all_gather(out_weight, 'ctx', axis=1, tiled=True)  131 us
    reduce_scatter x1, waiting for transfers between devices, on_device(): lax.psum_scatter(partial_sum.astype(jnp.bfloat16), 'tp', scatter_dimensio...  73.4 us
    ppermute x4, waiting for transfers between devices, from_behind(): return lax.ppermute(block, axis, route)  36.3 us
    ppermute x4, starting transfers between devices, from_behind(): return lax.ppermute(block, axis, route)  21.9 us
    dot_general x1, matrix products, on_device(): jnp.dot(attended, lax.all_gather(out_weight, 'ctx', axis=1, tiled=True),...  16.9 us
    dot_general x5, matrix products, advance(): jnp.einsum('kgtn,nkd->kgtd', prob.astype(jnp.bfloat16), value_block, pref...  15.6 us
    reduce_sum x5, other arithmetic, advance(): row_sum = row_sum * rescale + jnp.sum(prob, axis=-1)  10.2 us
    dot_general x5, matrix products, advance(): jnp.einsum('kgtd,nkd->kgtn', grouped, key_block, preferred_element_type=j...  8.2 us
  transfers between devices with their start and end apart: 6, of which 6 were waited for; matrix products, arithmetic and copies ran while one was open for 16% of the time, Pallas kernels for 0%

commit v1 on v0

v1 whole, which is shorter than its diff:
```python
import functools
import math

import jax
import jax.numpy as jnp
from jax import lax
from jax.experimental import pallas as pl
from jax.experimental.pallas import tpu as pltpu
from jax.sharding import PartitionSpec as P

HD = 128
DOC = 2048

theta_base = 1000000.0
MESH_ID = pl.DeviceIdType.MESH


def rotary_tables(positions):
    half_dim = HD // 2
    freq_index = jnp.arange(half_dim)
    inv_freq = theta_base ** (-2.0 * freq_index.astype(jnp.float32) / HD)
    first_end = HD // 8
    second_end = first_end + 3 * HD // 16
    place = positions.astype(jnp.float32)
    chosen = jnp.where(
        freq_index[None, :] < first_end,
        place[0][:, None],
        jnp.where(freq_index[None, :] < second_end, place[1][:, None], place[2][:, None]),
    )
    angle = chosen * inv_freq[None, :]
    return (jnp.cos(angle), jnp.sin(angle))


def rotate(vectors, cosine_table, sine_table):
    half_dim = HD // 2
    lower_half = vectors[..., :half_dim]
    upper_half = vectors[..., half_dim:]
    cos_b = cosine_table[:, None, :]
    sin_b = sine_table[:, None, :]
    return jnp.concatenate(
        [lower_half * cos_b - upper_half * sin_b, upper_half * cos_b + lower_half * sin_b], axis=-1
    )


def fused(
    n, inner, reach, tile,
    q_ref, kv_ref, start_ref, w_ref, out_ref,
    kvbuf, wbuf, abuf, bbuf, bias, xsend, xrecv, osend,
    kv_s, kv_r, w_s, w_r, a_s, a_r, f_s, b_r, x_s, x_r, o_s, o_r,
):
    outer = n // inner
    half = inner // 2
    tok = q_ref.shape[0]
    pairs = q_ref.shape[1] // (2 * HD)
    tiles = tok // tile
    span = reach * tok + tile
    rows = tok // 2
    quarter = rows // 2
    cols = w_ref.shape[1]
    c = lax.axis_index("ctx")
    t = lax.axis_index("tp")
    co, ci = c // inner, c % inner
    x, h = t // 2, t % 2
    other_x = 1 - x
    mate = {"ctx": c, "tp": 2 * x + 1 - h}
    across = {"ctx": c, "tp": 2 * other_x + h}

    def remote(src, dst, send, recv, device):
        return pltpu.make_async_remote_copy(
            src_ref=src, dst_ref=dst, send_sem=send, recv_sem=recv,
            device_id=device, device_id_type=MESH_ID,
        )

    def landed(dst, sem):
        pltpu.make_async_copy(dst, dst, sem).wait()

    barrier = pltpu.get_barrier_semaphore()

    def greet(device):
        pl.semaphore_signal(barrier, inc=1, device_id=device, device_id_type=MESH_ID)

    for d in range(1, reach + 1):
        @pl.when(c + d < n)
        def _():
            greet({"ctx": c + d, "tp": t})

        @pl.when(c >= d)
        def _():
            greet({"ctx": c - d, "tp": t})
    for d in range(1, inner):
        for g in range(2):
            greet({"ctx": co * inner + (ci + d) % inner, "tp": 2 * x + g})
    for d in range(1, outer):
        for g in range(2):
            greet({"ctx": (co + d) % outer * inner + ci, "tp": 2 * x + g})
    greet(mate)
    greet(across)
    near = jnp.minimum(reach, n - 1 - c) + jnp.minimum(reach, c)
    pl.semaphore_wait(barrier, near + 2 * (inner - 1) + 2 * (outer - 1) + 2)

    def kv_slot(d):
        return kvbuf.at[:, pl.ds((reach - d) * tok, tok), :]

    def kv_copy(d):
        return remote(kv_ref, kv_slot(d), kv_s.at[d - 1], kv_r.at[d - 1], {"ctx": c + d, "tp": t})

    for d in range(1, reach + 1):
        @pl.when(c + d < n)
        def _():
            kv_copy(d).start()

    owner = ci // half
    w_slot = wbuf.at[h, ci % half]
    w_sem = w_r.at[h, ci % half]

    def w_copy(d):
        device = {"ctx": co * inner + (ci + d) % inner, "tp": 2 * x + owner}
        return remote(w_ref, w_slot, w_s.at[d], w_sem, device)

    for d in range(1, inner):
        w_copy(d).start()

    @pl.when(owner != h)
    def _():
        w_copy(0).start()

    @pl.when(owner == h)
    def _():
        pltpu.make_async_copy(w_ref, w_slot, w_sem).start()

    kvbuf[:, reach * tok:, :] = kv_ref[...]
    for d in range(1, reach + 1):
        @pl.when(c < d)
        def _():
            kvbuf[:, (reach - d) * tok:(reach - d + 1) * tok, :] = jnp.zeros(kv_ref.shape, kv_ref.dtype)

    def fill_bias(rt, _):
        first = start_ref[pl.ds(pl.multiple_of(rt * tile, tile), tile), :] - (
            (c - reach) * tok + rt * tile
        )
        key = lax.broadcasted_iota(jnp.int32, (tile, span), 1)
        query = lax.broadcasted_iota(jnp.int32, (tile, span), 0) + reach * tok
        bias[rt] = jnp.where((key <= query) & (key >= first), 0.0, -1e30).astype(jnp.float32)
        return 0

    lax.fori_loop(0, tiles, fill_bias, 0)

    for d in range(1, reach + 1):
        @pl.when(c >= d)
        def _():
            landed(kv_slot(d), kv_r.at[d - 1])

    factor = math.log2(math.e) / math.sqrt(HD)

    def a_copy(d, hp):
        device = {"ctx": (co + d) % outer * inner + ci, "tp": t}
        return remote(abuf.at[co, hp], abuf.at[co, hp], a_s.at[d, hp], a_r.at[co, hp], device)

    def f_copy(slot, hp):
        return remote(abuf.at[slot, hp], bbuf.at[slot, hp], f_s.at[slot, hp], b_r.at[slot, hp], mate)

    def attend(hp, _):
        def one_tile(rt, _):
            at = pl.ds(pl.multiple_of(rt * tile, tile), tile)
            window = pl.ds(pl.multiple_of(rt * tile, tile), span)
            k = kvbuf[0, window, :]
            v = kvbuf[1, window, :]
            q2 = q_ref[at, pl.ds(pl.multiple_of(hp * 2 * HD, 2 * HD), 2 * HD)]
            done = []
            for e in range(2):
                q = q2[:, e * HD:(e + 1) * HD]
                s = lax.dot_general(
                    q, k, (((1,), (1,)), ((), ())), preferred_element_type=jnp.float32
                ) + bias[rt]
                peak = jnp.max(s, axis=-1, keepdims=True)
                p = jnp.exp2((s - peak) * factor)
                total = jnp.sum(p, axis=-1, keepdims=True)
                mixed = jnp.dot(p.astype(jnp.bfloat16), v, preferred_element_type=jnp.float32)
                done.append((mixed / total).astype(jnp.bfloat16))
            abuf[co, hp, at, :] = jnp.concatenate(done, axis=1)
            return 0

        lax.fori_loop(0, tiles, one_tile, 0)
        for d in range(1, outer):
            a_copy(d, hp).start()
        f_copy(co, hp).start()
        return 0

    lax.fori_loop(0, pairs, attend, 0)

    for i in range(half):
        landed(wbuf.at[0, i], w_r.at[0, i])
        landed(wbuf.at[1, i], w_r.at[1, i])

    def x_copy(slot):
        return remote(xsend.at[slot], xrecv.at[slot], x_s.at[slot], x_r.at[slot], across)

    def o_copy(slot, g):
        device = {"ctx": slot * inner + ci, "tp": 2 * x + g}
        return remote(osend.at[slot, g], out_ref.at[co, h], o_s.at[slot, g], o_r.at[co, h], device)

    def product(slot, side, i):
        at = pl.ds(pl.multiple_of(side * rows, rows), rows)
        mine = jnp.concatenate([abuf[slot, p, at, :] for p in range(pairs)], axis=1)
        theirs = jnp.concatenate([bbuf[slot, p, at, :] for p in range(pairs)], axis=1)
        return jnp.dot(mine, wbuf[h, i], preferred_element_type=jnp.float32) + jnp.dot(
            theirs, wbuf[1 - h, i], preferred_element_type=jnp.float32
        )

    def step(k, _):
        @pl.when((k >= 1) & (k < outer))
        def _():
            slot = (co + k) % outer

            def forward(hp, _):
                landed(abuf.at[slot, hp], a_r.at[slot, hp])
                f_copy(slot, hp).start()
                return 0

            lax.fori_loop(0, pairs, forward, 0)

        @pl.when((k >= 1) & (k <= outer))
        def _():
            slot = (co + k + outer - 1) % outer

            def arrive(hp, _):
                landed(bbuf.at[slot, hp], b_r.at[slot, hp])
                return 0

            lax.fori_loop(0, pairs, arrive, 0)
            for i in range(half):
                xsend[slot, :, i * cols:(i + 1) * cols] = product(slot, other_x, i).astype(jnp.bfloat16)
            x_copy(slot).start()

        @pl.when(k >= 2)
        def _():
            slot = (co + k + outer - 2) % outer
            landed(xrecv.at[slot], x_r.at[slot])
            for i in range(half):
                at = slice(i * cols, (i + 1) * cols)
                both = (product(slot, x, i) + xrecv[slot, :, at].astype(jnp.float32)).astype(jnp.bfloat16)
                osend[slot, 0, :, at] = both[:quarter]
                osend[slot, 1, :, at] = both[quarter:]
            for g in range(2):
                @pl.when((slot != co) | (h != g))
                def _():
                    o_copy(slot, g).start()

                @pl.when((slot == co) & (h == g))
                def _():
                    out_ref[co, h] = osend[slot, g]
        return 0

    lax.fori_loop(0, outer + 2, step, 0)

    for d in range(1, reach + 1):
        @pl.when(c + d < n)
        def _():
            kv_copy(d).wait_send()
    for d in range(1, inner):
        w_copy(d).wait_send()

    @pl.when(owner != h)
    def _():
        w_copy(0).wait_send()

    def drain(slot, _):
        def sent(hp, _):
            f_copy(slot, hp).wait_send()

            @pl.when(slot >= 1)
            def _():
                a_copy(slot, hp).wait_send()
            return 0

        lax.fori_loop(0, pairs, sent, 0)
        x_copy(slot).wait_send()
        for g in range(2):
            @pl.when((slot != co) | (h != g))
            def _():
                o_copy(slot, g).wait_send()
                landed(out_ref.at[slot, g], o_r.at[slot, g])
        return 0

    lax.fori_loop(0, outer, drain, 0)


def on_device(queries, keys, values, positions, segment_ids, out_weight, residual):
    tok = queries.shape[0]
    heads = queries.shape[1] // HD
    n = lax.axis_size("ctx")
    inner = 2 ** max(1, int(math.log2(n)) // 2)
    outer = n // inner
    half = inner // 2
    reach = (DOC + tok - 2) // tok
    tile = math.gcd(tok, 256)
    my_start = lax.axis_index("ctx") * tok
    depth, cols = out_weight.shape
    cosine_table, sine_table = rotary_tables(positions)
    rot_q = rotate(
        queries.reshape(tok, heads, HD).astype(jnp.float32), cosine_table, sine_table
    ).astype(jnp.bfloat16).reshape(tok, heads * HD)
    rot_k = rotate(
        keys.reshape(tok, 1, HD).astype(jnp.float32), cosine_table, sine_table
    ).astype(jnp.bfloat16).reshape(tok, HD)
    pair = jnp.stack([rot_k, values], axis=0)
    my_seg = lax.dynamic_slice_in_dim(segment_ids, my_start, tok, 0)
    start = jnp.sum((segment_ids[None, :] < my_seg[:, None]).astype(jnp.int32), axis=1, keepdims=True)
    pairs = heads // 2
    rows = tok // 2
    wide = half * cols
    bf16 = jnp.bfloat16
    dma = pltpu.SemaphoreType.DMA
    vmem = pl.BlockSpec(memory_space=pltpu.VMEM)
    gathered = pl.pallas_call(
        functools.partial(fused, n, inner, reach, tile),
        out_shape=jax.ShapeDtypeStruct((outer, 2, rows // 2, wide), bf16),
        in_specs=[vmem] * 4,
        out_specs=vmem,
        scratch_shapes=[
            pltpu.VMEM((2, (reach + 1) * tok, HD), bf16),
            pltpu.VMEM((2, half, depth, cols), bf16),
            pltpu.VMEM((outer, pairs, tok, 2 * HD), bf16),
            pltpu.VMEM((outer, pairs, tok, 2 * HD), bf16),
            pltpu.VMEM((tok // tile, tile, reach * tok + tile), jnp.float32),
            pltpu.VMEM((outer, rows, wide), bf16),
            pltpu.VMEM((outer, rows, wide), bf16),
            pltpu.VMEM((outer, 2, rows // 2, wide), bf16),
            dma((reach,)), dma((reach,)),
            dma((inner,)), dma((2, half)),
            dma((outer, pairs)), dma((outer, pairs)),
            dma((outer, pairs)), dma((outer, pairs)),
            dma((outer,)), dma((outer,)),
            dma((outer, 2)), dma((outer, 2)),
        ],
        compiler_params=pltpu.CompilerParams(
            collective_id=0, has_side_effects=True, vmem_limit_bytes=60 * 1024 * 1024
        ),
    )(rot_q, pair, start, out_weight)
    shared = gathered.transpose(2, 0, 1, 3).reshape(residual.shape)
    return (shared.astype(jnp.float32) + residual.astype(jnp.float32)).astype(jnp.bfloat16)


def solution(mesh):
    return jax.shard_map(
        on_device,
        mesh=mesh,
        in_specs=(
            P("ctx", "tp"),
            P("ctx", "tp"),
            P("ctx", "tp"),
            P(None, "ctx"),
            P(),
            P("tp", "ctx"),
            P(("ctx", "tp"), None),
        ),
        out_specs=P(("ctx", "tp"), None),
        check_vma=False,
    )
```

time: 361 us -> 228 us (0.63)
  waiting for transfers between devices: 242 us -> 0 us
  Pallas kernels: 0 us -> 196 us
  matrix products: 40.7 us -> 0 us
  starting transfers between devices: 21.9 us -> 0 us
  between operations: 13.6 us -> 0.08 us
  other arithmetic: 24.4 us -> 17 us
    pallas_call x0 -> x1, Pallas kernels: none -> 196 us  [on_device(): pl.pallas_call(functools.partial(fused, n, inner, reach, tile), out_shape...]
    all_gather x1 -> x0, waiting for transfers between devices: 131 us -> none  [on_device(): lax.all_gather(out_weight, 'ctx', axis=1, tiled=True)]
    reduce_scatter x1 -> x0, waiting for transfers between devices: 73.4 us -> none  [on_device(): lax.psum_scatter(partial_sum.astype(jnp.bfloat16), 'tp', scatter_dimensio...]
    dot_general x11 -> x0, matrix products: 40.7 us -> none  [the longest x1 16.9 us: on_device(): jnp.dot(attended, lax.all_gather(out_weight, 'ctx', axis=1, tiled=True),...]
    ppermute x4 -> x0, waiting for transfers between devices: 36.3 us -> none  [from_behind(): return lax.ppermute(block, axis, route)]
    ppermute x4 -> x0, starting transfers between devices: 21.9 us -> none  [from_behind(): return lax.ppermute(block, axis, route)]
    reduce_sum x5 -> x1, other arithmetic: 10.2 us -> 1.68 us  [on_device(): jnp.sum((segment_ids[None, :] < my_seg[:, None]).astype(jnp.int32), axis=...]
    convert_element_type x0 -> x2, local copies, waits for them, and re-layouts: none -> 8.38 us  [the longest x1 5.49 us: on_device(): shared.astype(jnp.float32) + residual.astype(jnp.float32)]
  transfers between devices with their start and end apart: 6 -> 0, of which waited for: 6 -> 0; matrix products, arithmetic and copies ran while one was open for 16% -> 0% of each run, Pallas kernels for 0% -> 0%
where the time goes in v1:
time: 228 us; the launch traced here: 227 us
  Pallas kernels  196 us (86%)
  other arithmetic  17 us (7%)
  local copies, waits for them, and re-layouts  14.2 us (6%)
    pallas_call x1, Pallas kernels, on_device(): pl.pallas_call(functools.partial(fused, n, inner, reach, tile), out_shape...  196 us
    convert_element_type x1, local copies, waits for them, and re-layouts, on_device(): shared.astype(jnp.float32) + residual.astype(jnp.float32)  5.49 us

profile of v1, /device:TPU:5, one launch (start us, length us, event | category | flops | bytes accessed | tf_op | source)
XLA Modules:
  0.0 227.2 jit_solution(3737881531301845233)
XLA Ops:
  0.0 0.0 copy-start.1
  0.0 0.8 dynamic_slice.3
  0.9 1.7 convert_reduce_fusion
  2.6 0.7 convert_element_type.59
  3.3 0.9 copy.12.start_ref
  4.1 0.9 bitcast_convert_fusion
  5.1 1.4 fusion.5
  6.5 1.7 pad_maximum_fusion.1.kv_ref
  8.2 1.7 fusion.4
  9.9 0.0 copy-done.1
  9.9 0.2 convert_bitcast_fusion.1
  10.1 0.5 copy.16
  10.6 0.8 subtract_convert_fusion
  11.4 0.6 pad_maximum_fusion
  12.0 1.2 copy.19
  13.2 195.9 %shard_map.73 = bf16[4,2,128,1024]{3,2,1,0:T(8,128)(2,1)} custom-call(bf16[512,1024]{1,0:T(8,128)(2,1)} %bitcast.27, bf16[2,512,128]{2,1,0:T(8,128)(2,1)} %pad_maximum_fusion.1.kv_ref, s32[512,1]{1,0:T(8,128)} %copy.12.start_ref, bf16[1024,1024]{1,0:T(8,128)(2,1)} %w_ref.1), custom_call_target="tpu_custom_call" | custom-call | tf_op jit(solution)/shard_map/pallas_call | solution.py:315
  209.1 4.0 %convert_bitcast_fusion = f32[128,4,2,1024]{3,0,2,1:T(8,128)} fusion(bf16[4,2,128,1024]{3,2,1,0:T(8,128)(2,1)} %shard_map.73), kind=kLoop, calls=%fused_computation.3 | loop fusion | flops 1048576 | bytes 6291456 | tf_op jit(solution)/shard_map/convert_element_type | solution.py:341
  213.1 0.0 copy-start
  213.1 5.5 %copy.13 = f32[128,4,2,1024]{0,3,2,1:T(8,128)} copy(f32[128,4,2,1024]{3,0,2,1:T(8,128)} %convert_bitcast_fusion) | data formatting | bytes 8388608 | tf_op jit(solution)/shard_map/convert_element_type | solution.py:341
  218.6 0.0 copy-done
  218.6 2.4 %copy.14 = bf16[128,8192]{0,1:T(8,128)(2,1)} copy(bf16[128,8192]{1,0:T(8,128)(2,1)S(1)} %copy-done) | data formatting | bytes 4194304 | tf_op args[6]
  221.0 3.3 %fusion = bf16[128,8192]{0,1:T(8,128)(2,1)S(1)} fusion(f32[128,4,2,1024]{0,3,2,1:T(8,128)} %copy.13, bf16[128,8192]{0,1:T(8,128)(2,1)} %copy.14), kind=kLoop, calls=%fused_computation.2 | loop fusion | flops 3145728 | bytes 8388608 | tf_op jit(solution)/shard_map/convert_element_type | solution.py:341
  224.3 2.9 %copy.15 = bf16[128,8192]{1,0:T(8,128)(2,1)} copy(bf16[128,8192]{0,1:T(8,128)(2,1)S(1)} %fusion) | data formatting | bytes 4194304 | tf_op jit(solution)/shard_map/convert_element_type | solution.py:341
  (3 shorter events, 0.0 us)
Async XLA Ops:
  0.0 9.9 %copy-start.1 = (bf16[512,1024]{1,0:T(8,128)(2,1)S(1)}, bf16[512,1024]{1,0:T(8,128)(2,1)}, u32[]{:S(2)}) copy-start(bf16[512,1024]{1,0:T(8,128)(2,1)} %param.7) | copy-start | bytes 3145732
  213.1 5.5 %copy-start = (bf16[128,8192]{1,0:T(8,128)(2,1)S(1)}, bf16[128,8192]{1,0:T(8,128)(2,1)}, u32[]{:S(2)}) copy-start(bf16[128,8192]{1,0:T(8,128)(2,1)} %param.13) | copy-start | bytes 6291460

commit v2 on v1

--- a/solution.py
+++ b/solution.py
@@ -46,7 +46,7 @@
     n, inner, reach, tile,
     q_ref, kv_ref, start_ref, w_ref, out_ref,
     kvbuf, wbuf, abuf, bbuf, bias, xsend, xrecv, osend,
-    kv_s, kv_r, w_s, w_r, a_s, a_r, f_s, b_r, x_s, x_r, o_s, o_r,
+    kv_s, kv_r, w_s, w_r, up_s, down_s, a_r, f_s, b_r, x_s, x_r, o_s, o_r,
 ):
     outer = n // inner
     half = inner // 2
@@ -152,12 +152,42 @@
 
     factor = math.log2(math.e) / math.sqrt(HD)
 
-    def a_copy(d, hp):
-        device = {"ctx": (co + d) % outer * inner + ci, "tp": t}
-        return remote(abuf.at[co, hp], abuf.at[co, hp], a_s.at[d, hp], a_r.at[co, hp], device)
+    def up_copy(slot, hp):
+        device = {"ctx": c + inner, "tp": t}
+        return remote(abuf.at[slot, hp], abuf.at[slot, hp], up_s.at[slot, hp], a_r.at[slot, hp], device)
+
+    def down_copy(slot, hp):
+        device = {"ctx": c - inner, "tp": t}
+        return remote(abuf.at[slot, hp], abuf.at[slot, hp], down_s.at[slot, hp], a_r.at[slot, hp], device)
 
     def f_copy(slot, hp):
         return remote(abuf.at[slot, hp], bbuf.at[slot, hp], f_s.at[slot, hp], b_r.at[slot, hp], mate)
+
+    def pass_on(slot, hp):
+        @pl.when((slot <= co) & (co + 1 < outer))
+        def _():
+            up_copy(slot, hp).start()
+
+        @pl.when((slot >= co) & (co >= 1))
+        def _():
+            down_copy(slot, hp).start()
+
+        f_copy(slot, hp).start()
+
+    def forward(slot, hp):
+        landed(abuf.at[slot, hp], a_r.at[slot, hp])
+        pass_on(slot, hp)
+
+    def each_side(distance, action):
+        def one_side(side, _):
+            slot = co + distance * (2 * side - 1)
+
+            @pl.when((slot >= 0) & (slot < outer) & ((distance > 0) | (side == 1)))
+            def _():
+                action(slot)
+            return 0
+
+        lax.fori_loop(0, 2, one_side, 0)
 
     def attend(hp, _):
         def one_tile(rt, _):
@@ -181,11 +211,14 @@
             return 0
 
         lax.fori_loop(0, tiles, one_tile, 0)
-        for d in range(1, outer):
-            a_copy(d, hp).start()
-        f_copy(co, hp).start()
+        pass_on(co, hp)
+
+        @pl.when(hp >= lag)
+        def _():
+            each_side(1, lambda slot: forward(slot, hp - lag))
         return 0
 
+    lag = min(2, pairs)
     lax.fori_loop(0, pairs, attend, 0)
 
     for i in range(half):
@@ -195,9 +228,14 @@
     def x_copy(slot):
         return remote(xsend.at[slot], xrecv.at[slot], x_s.at[slot], x_r.at[slot], across)
 
+    wide = out_ref.shape[1] // (2 * outer)
+
+    def out_slot(slot, g):
+        return out_ref.at[:, pl.ds(pl.multiple_of((slot * 2 + g) * wide, 128), wide)]
+
     def o_copy(slot, g):
         device = {"ctx": slot * inner + ci, "tp": 2 * x + g}
-        return remote(osend.at[slot, g], out_ref.at[co, h], o_s.at[slot, g], o_r.at[co, h], device)
+        return remote(osend.at[slot, g], out_slot(co, h), o_s.at[slot, g], o_r.at[co, h], device)
 
     def product(slot, side, i):
         at = pl.ds(pl.multiple_of(side * rows, rows), rows)
@@ -207,51 +245,49 @@
             theirs, wbuf[1 - h, i], preferred_element_type=jnp.float32
         )
 
-    def step(k, _):
-        @pl.when((k >= 1) & (k < outer))
-        def _():
-            slot = (co + k) % outer
-
-            def forward(hp, _):
-                landed(abuf.at[slot, hp], a_r.at[slot, hp])
-                f_copy(slot, hp).start()
+    def send_product(slot):
+        def arrive(hp, _):
+            landed(bbuf.at[slot, hp], b_r.at[slot, hp])
+            return 0
+
+        lax.fori_loop(0, pairs, arrive, 0)
+        for i in range(half):
+            xsend[slot, :, i * cols:(i + 1) * cols] = product(slot, other_x, i).astype(jnp.bfloat16)
+        x_copy(slot).start()
+
+    def add_product(slot):
+        landed(xrecv.at[slot], x_r.at[slot])
+        for i in range(half):
+            at = slice(i * cols, (i + 1) * cols)
+            both = (product(slot, x, i) + xrecv[slot, :, at].astype(jnp.float32)).astype(jnp.bfloat16)
+            osend[slot, 0, :, at] = both[:quarter]
+            osend[slot, 1, :, at] = both[quarter:]
+        for g in range(2):
+            @pl.when((slot != co) | (h != g))
+            def _():
+                o_copy(slot, g).start()
+
+            @pl.when((slot == co) & (h == g))
+            def _():
+                out_ref[:, pl.ds(pl.multiple_of((co * 2 + h) * wide, 128), wide)] = osend[slot, g]
+
+    def step(d, _):
+        each_side(d - 1, send_product)
+
+        def rest(slot):
+            first = jnp.where(d == 1, pairs - lag, 0)
+
+            def one(hp, _):
+                forward(slot, hp)
                 return 0
 
-            lax.fori_loop(0, pairs, forward, 0)
-
-        @pl.when((k >= 1) & (k <= outer))
-        def _():
-            slot = (co + k + outer - 1) % outer
-
-            def arrive(hp, _):
-                landed(bbuf.at[slot, hp], b_r.at[slot, hp])
-                return 0
-
-            lax.fori_loop(0, pairs, arrive, 0)
-            for i in range(half):
-                xsend[slot, :, i * cols:(i + 1) * cols] = product(slot, other_x, i).astype(jnp.bfloat16)
-            x_copy(slot).start()
-
-        @pl.when(k >= 2)
-        def _():
-            slot = (co + k + outer - 2) % outer
-            landed(xrecv.at[slot], x_r.at[slot])
-            for i in range(half):
-                at = slice(i * cols, (i + 1) * cols)
-                both = (product(slot, x, i) + xrecv[slot, :, at].astype(jnp.float32)).astype(jnp.bfloat16)
-                osend[slot, 0, :, at] = both[:quarter]
-                osend[slot, 1, :, at] = both[quarter:]
-            for g in range(2):
-                @pl.when((slot != co) | (h != g))
-                def _():
-                    o_copy(slot, g).start()
-
-                @pl.when((slot == co) & (h == g))
-                def _():
-                    out_ref[co, h] = osend[slot, g]
+            lax.fori_loop(first, pairs, one, 0)
+
+        each_side(d, rest)
+        each_side(d - 1, add_product)
         return 0
 
-    lax.fori_loop(0, outer + 2, step, 0)
+    lax.fori_loop(1, outer + 1, step, 0)
 
     for d in range(1, reach + 1):
         @pl.when(c + d < n)
@@ -268,9 +304,13 @@
         def sent(hp, _):
             f_copy(slot, hp).wait_send()
 
-            @pl.when(slot >= 1)
-            def _():
-                a_copy(slot, hp).wait_send()
+            @pl.when((slot <= co) & (co + 1 < outer))
+            def _():
+                up_copy(slot, hp).wait_send()
+
+            @pl.when((slot >= co) & (co >= 1))
+            def _():
+                down_copy(slot, hp).wait_send()
             return 0
 
         lax.fori_loop(0, pairs, sent, 0)
@@ -279,7 +319,7 @@
             @pl.when((slot != co) | (h != g))
             def _():
                 o_copy(slot, g).wait_send()
-                landed(out_ref.at[slot, g], o_r.at[slot, g])
+                landed(out_slot(slot, g), o_r.at[slot, g])
         return 0
 
     lax.fori_loop(0, outer, drain, 0)
@@ -314,7 +354,7 @@
     vmem = pl.BlockSpec(memory_space=pltpu.VMEM)
     gathered = pl.pallas_call(
         functools.partial(fused, n, inner, reach, tile),
-        out_shape=jax.ShapeDtypeStruct((outer, 2, rows // 2, wide), bf16),
+        out_shape=jax.ShapeDtypeStruct((rows // 2, outer * 2 * wide), bf16),
         in_specs=[vmem] * 4,
         out_specs=vmem,
         scratch_shapes=[
@@ -328,6 +368,7 @@
             pltpu.VMEM((outer, 2, rows // 2, wide), bf16),
             dma((reach,)), dma((reach,)),
             dma((inner,)), dma((2, half)),
+            dma((outer, pairs)),
             dma((outer, pairs)), dma((outer, pairs)),
             dma((outer, pairs)), dma((outer, pairs)),
             dma((outer,)), dma((outer,)),
@@ -337,8 +378,7 @@
             collective_id=0, has_side_effects=True, vmem_limit_bytes=60 * 1024 * 1024
         ),
     )(rot_q, pair, start, out_weight)
-    shared = gathered.transpose(2, 0, 1, 3).reshape(residual.shape)
-    return (shared.astype(jnp.float32) + residual.astype(jnp.float32)).astype(jnp.bfloat16)
+    return (gathered.astype(jnp.float32) + residual.astype(jnp.float32)).astype(jnp.bfloat16)
 
 
 def solution(mesh):

time: 228 us -> 161 us (0.71)
  Pallas kernels: 196 us -> 146 us
  local copies, waits for them, and re-layouts: 14.2 us -> 2.7 us
  other arithmetic: 17 us -> 11.9 us
    pallas_call x1, Pallas kernels: 196 us -> 146 us  [on_device(): pl.pallas_call(functools.partial(fused, n, inner, reach, tile), out_shape...]
    convert_element_type x2 -> x0, local copies, waits for them, and re-layouts: 8.38 us -> none  [the longest x1 5.49 us: on_device(): shared.astype(jnp.float32) + residual.astype(jnp.float32)]
    convert_element_type x2 -> x1, other arithmetic: 7.27 us -> 3.41 us  [on_device(): (gathered.astype(jnp.float32) + residual.astype(jnp.float32)).astype(jnp....]
    unnamed x7 -> x10, local copies, waits for them, and re-layouts: 4.14 us -> 1.74 us
where the time goes in v2:
time: 161 us; the launch traced here: 160 us
  Pallas kernels  146 us (91%)
  other arithmetic  11.9 us (7%)
  local copies, waits for them, and re-layouts  2.7 us (2%)
    pallas_call x1, Pallas kernels, on_device(): pl.pallas_call(functools.partial(fused, n, inner, reach, tile), out_shape...  146 us
    convert_element_type x1, other arithmetic, on_device(): (gathered.astype(jnp.float32) + residual.astype(jnp.float32)).astype(jnp....  3.41 us

profile of v2, /device:TPU:5, one launch (start us, length us, event | category | flops | bytes accessed | tf_op | source)
XLA Modules:
  0.0 160.5 jit_solution(17442838525612214493)
XLA Ops:
  0.0 0.7 convert_element_type.53
  0.7 1.7 %fusion.3 = (f32[512,64]{1,0:T(8,128)S(1)}, f32[512,64]{1,0:T(8,128)S(1)}) fusion(f32[64]{0:T(128)S(1)} %multiply_power_fusion, f32[512]{0:T(512)S(1)} %bitcast.25, f32[512]{0:T(512)S(1)} %bitcast.27, f32[512]{0:T(512)S(1)} %bitcast.23, pred[64]{0:T(512)(128)(4,1)S(1)} %get-tuple-element.14, pred[64]{0:T(512)(128)(4,1)S(1)} %get-tuple-element.15), kind=kLoop, calls=%fused_computation.15 | loop fusion | flops 98304 | bytes 268672 | tf_op jit(solution)/shard_map/cos | solution.py:31
  2.4 1.5 convert_bitcast_fusion
  3.9 0.5 copy.10
  4.4 0.8 subtract_convert_fusion
  5.2 0.0 copy-start.1
  5.2 0.6 pad_maximum_fusion
  5.8 0.0 copy-start.2
  5.8 0.0 copy-start.3
  5.8 1.2 copy.13
  7.1 0.0 copy-done.1
  7.1 1.4 fusion.4
  8.5 0.0 copy-done.2
  8.5 0.8 pad_maximum_fusion.1.kv_ref
  9.3 0.0 copy-done.3
  9.3 0.1 dynamic_slice.3
  9.4 1.0 convert_reduce_fusion
  10.4 0.9 copy.9.start_ref
  11.3 0.0 copy-start
  11.3 145.8 %shard_map.73 = bf16[128,8192]{1,0:T(8,128)(2,1)} custom-call(bf16[512,1024]{1,0:T(8,128)(2,1)} %bitcast.21, bf16[2,512,128]{2,1,0:T(8,128)(2,1)} %pad_maximum_fusion.1.kv_ref, s32[512,1]{1,0:T(8,128)} %copy.9.start_ref, bf16[1024,1024]{1,0:T(8,128)(2,1)} %w_ref.1), custom_call_target="tpu_custom_call" | custom-call | tf_op jit(solution)/shard_map/pallas_call | solution.py:355
  157.1 0.0 copy-done
  157.1 3.4 %add_convert_fusion = bf16[128,8192]{1,0:T(8,128)(2,1)} fusion(bf16[128,8192]{1,0:T(8,128)(2,1)S(1)} %copy-done, bf16[128,8192]{1,0:T(8,128)(2,1)} %shard_map.73), kind=kLoop, calls=%fused_computation.1 | loop fusion | flops 4194304 | bytes 6291456 | tf_op jit(solution)/shard_map/convert_element_type | solution.py:381
  (4 shorter events, 0.0 us)
Async XLA Ops:
  5.2 1.9 %copy-start.1 = (bf16[512,128]{1,0:T(8,128)(2,1)S(1)}, bf16[512,128]{1,0:T(8,128)(2,1)}, u32[]{:S(2)}) copy-start(bf16[512,128]{1,0:T(8,128)(2,1)} %param.8) | copy-start | bytes 393220
  5.8 2.7 %copy-start.2 = (bf16[512,128]{1,0:T(8,128)(2,1)S(1)}, bf16[512,128]{1,0:T(8,128)(2,1)}, u32[]{:S(2)}) copy-start(bf16[512,128]{1,0:T(8,128)(2,1)} %param.9) | copy-start | bytes 393220
  5.8 3.5 %copy-start.3 = (s32[4096]{0:T(1024)S(1)}, s32[4096]{0:T(1024)}, u32[]{:S(2)}) copy-start(s32[4096]{0:T(1024)} %param.11) | copy-start | bytes 49156
  11.3 145.8 %copy-start = (bf16[128,8192]{1,0:T(8,128)(2,1)S(1)}, bf16[128,8192]{1,0:T(8,128)(2,1)}, u32[]{:S(2)}) copy-start(bf16[128,8192]{1,0:T(8,128)(2,1)} %param.13) | copy-start | bytes 6291460

commit v3 on v2

--- a/solution.py
+++ b/solution.py
@@ -218,7 +218,7 @@
             each_side(1, lambda slot: forward(slot, hp - lag))
         return 0
 
-    lag = min(2, pairs)
+    lag = min(1, pairs)
     lax.fori_loop(0, pairs, attend, 0)
 
     for i in range(half):

time: 161 us -> 164 us (1.019)
  Pallas kernels: 146 us -> 150 us
    pallas_call x1, Pallas kernels: 146 us -> 150 us  [on_device(): pl.pallas_call(functools.partial(fused, n, inner, reach, tile), out_shape...]
where the time goes in v3:
time: 164 us
  Pallas kernels  150 us (91%)
  other arithmetic  11.9 us (7%)
  local copies, waits for them, and re-layouts  2.7 us (2%)
    pallas_call x1, Pallas kernels, on_device(): pl.pallas_call(functools.partial(fused, n, inner, reach, tile), out_shape...  150 us
    convert_element_type x1, other arithmetic, on_device(): (gathered.astype(jnp.float32) + residual.astype(jnp.float32)).astype(jnp....  3.41 us

profile of v3, /device:TPU:5, one launch (start us, length us, event | category | flops | bytes accessed | tf_op | source)
XLA Modules:
  0.0 164.3 jit_solution(12473622874056984646)
XLA Ops:
  0.0 0.7 convert_element_type.53
  0.7 1.7 %fusion.3 = (f32[512,64]{1,0:T(8,128)S(1)}, f32[512,64]{1,0:T(8,128)S(1)}) fusion(f32[64]{0:T(128)S(1)} %multiply_power_fusion, f32[512]{0:T(512)S(1)} %bitcast.25, f32[512]{0:T(512)S(1)} %bitcast.27, f32[512]{0:T(512)S(1)} %bitcast.23, pred[64]{0:T(512)(128)(4,1)S(1)} %get-tuple-element.14, pred[64]{0:T(512)(128)(4,1)S(1)} %get-tuple-element.15), kind=kLoop, calls=%fused_computation.15 | loop fusion | flops 98304 | bytes 268672 | tf_op jit(solution)/shard_map/cos | solution.py:31
  2.4 1.5 convert_bitcast_fusion
  3.9 0.5 copy.10
  4.4 0.8 subtract_convert_fusion
  5.2 0.0 copy-start.1
  5.2 0.6 pad_maximum_fusion
  5.8 0.0 copy-start.2
  5.8 0.0 copy-start.3
  5.8 1.2 copy.13
  7.1 0.0 copy-done.1
  7.1 1.4 fusion.4
  8.5 0.0 copy-done.2
  8.5 0.8 pad_maximum_fusion.1.kv_ref
  9.3 0.0 copy-done.3
  9.3 0.1 dynamic_slice.3
  9.4 1.0 convert_reduce_fusion
  10.4 0.9 copy.9.start_ref
  11.3 0.0 copy-start
  11.3 149.6 %shard_map.73 = bf16[128,8192]{1,0:T(8,128)(2,1)} custom-call(bf16[512,1024]{1,0:T(8,128)(2,1)} %bitcast.21, bf16[2,512,128]{2,1,0:T(8,128)(2,1)} %pad_maximum_fusion.1.kv_ref, s32[512,1]{1,0:T(8,128)} %copy.9.start_ref, bf16[1024,1024]{1,0:T(8,128)(2,1)} %w_ref.1), custom_call_target="tpu_custom_call" | custom-call | tf_op jit(solution)/shard_map/pallas_call | solution.py:355
  160.8 0.0 copy-done
  160.9 3.4 %add_convert_fusion = bf16[128,8192]{1,0:T(8,128)(2,1)} fusion(bf16[128,8192]{1,0:T(8,128)(2,1)S(1)} %copy-done, bf16[128,8192]{1,0:T(8,128)(2,1)} %shard_map.73), kind=kLoop, calls=%fused_computation.1 | loop fusion | flops 4194304 | bytes 6291456 | tf_op jit(solution)/shard_map/convert_element_type | solution.py:381
  (4 shorter events, 0.0 us)
Async XLA Ops:
  5.2 1.9 %copy-start.1 = (bf16[512,128]{1,0:T(8,128)(2,1)S(1)}, bf16[512,128]{1,0:T(8,128)(2,1)}, u32[]{:S(2)}) copy-start(bf16[512,128]{1,0:T(8,128)(2,1)} %param.8) | copy-start | bytes 393220
  5.8 2.7 %copy-start.2 = (bf16[512,128]{1,0:T(8,128)(2,1)S(1)}, bf16[512,128]{1,0:T(8,128)(2,1)}, u32[]{:S(2)}) copy-start(bf16[512,128]{1,0:T(8,128)(2,1)} %param.9) | copy-start | bytes 393220
  5.8 3.5 %copy-start.3 = (s32[4096]{0:T(1024)S(1)}, s32[4096]{0:T(1024)}, u32[]{:S(2)}) copy-start(s32[4096]{0:T(1024)} %param.11) | copy-start | bytes 49156
  11.3 149.6 %copy-start = (bf16[128,8192]{1,0:T(8,128)(2,1)S(1)}, bf16[128,8192]{1,0:T(8,128)(2,1)}, u32[]{:S(2)}) copy-start(bf16[128,8192]{1,0:T(8,128)(2,1)} %param.13) | copy-start | bytes 6291460
